TPU v7x, 32 devices: a whole 2x2x4 slice. The times are simulated.
32 devices in a mesh: tm: 8 (over z, x), pair: 4 (over y, core).
Axes of the slice: x: 2, y: 2, z: 4, core: 2. Of those that a mesh axis runs over, the one named last changes fastest.
Arguments:
- signal: float32 [2, 131072], P(None, 'tm'), may hold values from -6 to 6
- hop_offsets: int32 [2048], P(('tm', 'pair')), may hold values from 0 to 131071, as said below
- pair_channels: int32 [2, 8192], P(None, 'pair'), may hold values from 0 to 255
Outputs:
- surface: float32 [64, 8192], P(None, 'pair')
Inputs may be any that keep to these rules, and one draw needn't show every extreme that they name: `hop_offsets`: hop p starts at a sample in p * 64 to p * 64 + 63.
All inputs are finite; a program needn't handle non-finite values.
Results may differ from a plain program's by a relative error of at most 0.000071.
Values sent between devices are 32-bit elements; how exact they have to be, the bound alone decides.
A program may use at most 64 MiB of HBM per device.

v0:
```python
import math

import jax
import jax.numpy as jnp
from jax import lax
from jax.sharding import PartitionSpec as P

NP = 256
Q = 64
STRIDE = 64


def shifted(array, axis, by):
    devices = lax.axis_size(axis)
    pairs = [(i, i + by) for i in range(devices) if 0 <= i + by < devices]
    return lax.ppermute(array, axis, pairs)


def first_table():
    sample = jnp.arange(NP, dtype=jnp.int32)
    turns = sample[:, None] * sample[None, :] % NP
    angle = 2.0 * jnp.pi * turns.astype(jnp.float32) / NP
    window = 0.54 - 0.46 * jnp.cos(2.0 * jnp.pi * sample.astype(jnp.float32) / NP)
    gainval = 1.0 / jnp.sqrt(jnp.sum(window * window))
    weight = (window * gainval)[:, None]
    cosine = jnp.cos(angle) * weight
    sine = jnp.sin(angle) * weight
    upper = jnp.concatenate([cosine, -sine], axis=1)
    lower = jnp.concatenate([sine, cosine], axis=1)
    return jnp.concatenate([upper, lower], axis=0)


def second_table():
    sample = jnp.arange(Q, dtype=jnp.int32)
    turns = sample[:, None] * sample[None, :] % Q
    angle = 2.0 * jnp.pi * turns.astype(jnp.float32) / Q
    cosine = jnp.cos(angle) / math.sqrt(Q)
    sine = jnp.sin(angle) / math.sqrt(Q)
    upper = jnp.concatenate([cosine, sine], axis=1)
    lower = jnp.concatenate([-sine, cosine], axis=1)
    return jnp.concatenate([upper, lower], axis=0)


def cut_frames(extended, offsets, base):
    rows = offsets.shape[0]
    pieces = []
    for index in range(NP // STRIDE + 1):
        part_rows = extended[:, index * STRIDE : index * STRIDE + rows * STRIDE]
        pieces.append(part_rows.reshape(2, rows, STRIDE))
    segment = jnp.concatenate(pieces, axis=2)
    nominal = jnp.arange(rows, dtype=jnp.int32) * STRIDE
    jitter = offsets - base - nominal
    bit = 0
    while 1 << bit < STRIDE:
        step = 1 << bit
        moved = jnp.concatenate(
            [segment[:, :, step:], jnp.zeros((2, rows, step), segment.dtype)], axis=2
        )
        flagged = jitter >> bit & 1 == 1
        segment = jnp.where(flagged[None, :, None], moved, segment)
        bit = bit + 1
    return jnp.concatenate([segment[0, :, :NP], segment[1, :, :NP]], axis=1)


def channelize(extended, offsets, base):
    sample = jnp.arange(NP, dtype=jnp.int32)
    frames = cut_frames(extended, offsets, base)
    raw = jnp.dot(
        frames, first_table(), precision=lax.Precision.HIGHEST, preferred_element_type=jnp.float32
    )
    turns = sample[None, :] * (offsets[:, None] % NP) % NP
    theta = 2.0 * jnp.pi * turns.astype(jnp.float32) / NP
    cosine = jnp.cos(theta)
    sine = jnp.sin(theta)
    real_part = raw[:, :NP]
    imag_part = raw[:, NP:]
    return jnp.concatenate(
        [real_part * cosine + imag_part * sine, imag_part * cosine - real_part * sine], axis=1
    )


def two_sum(left, right):
    total = left[0] + right[0]
    back = total - left[0]
    error = left[0] - (total - back) + (right[0] - back)
    return (total, left[1] + error)


def shards(signal, hop_offsets, pair_channels):
    span = signal.shape[1]
    edge_part = shifted(signal[:, :NP], "tm", -1)
    extended = jnp.concatenate([signal, edge_part], axis=1)
    base = lax.axis_index("tm") * span
    all_offsets = lax.all_gather(hop_offsets, "pair", axis=0, tiled=True)
    spectra = channelize(extended, all_offsets, base)
    hop_count = spectra.shape[0]
    blocks = hop_count // Q
    local_pairs = pair_channels.shape[1]
    width = math.gcd(local_pairs, 512)
    grouped = pair_channels.reshape(2, local_pairs // width, width).transpose(1, 0, 2)
    table = second_table()
    channel_major = spectra.T

    def block_power(index):
        columns = jnp.concatenate([index[0], index[0] + NP, index[1], index[1] + NP])
        picked = jnp.take(channel_major, columns, axis=0)
        first_re = picked[:width]
        first_im = picked[width : 2 * width]
        second_re = picked[2 * width : 3 * width]
        second_im = picked[3 * width :]
        prod_re = first_re * second_re + first_im * second_im
        prod_im = first_im * second_re - first_re * second_im
        stacked = jnp.concatenate(
            [prod_re.reshape(width, blocks, Q), prod_im.reshape(width, blocks, Q)], axis=2
        )
        cyclic = jnp.einsum(
            "qh,pbh->pbq",
            table,
            stacked,
            precision=lax.Precision.HIGHEST,
            preferred_element_type=jnp.float32,
        )
        power = jnp.sum(cyclic * cyclic, axis=1)
        return power[:, :Q] + power[:, Q:]

    powers = lax.map(block_power, grouped)
    partial_power = powers.transpose(2, 0, 1).reshape(Q, local_pairs)
    devices = lax.axis_size("tm")
    total_blocks = blocks * devices
    received = lax.all_to_all(partial_power, "tm", split_axis=0, concat_axis=0, tiled=True)
    pieces = received.reshape(devices, Q // devices, local_pairs)
    zeros = jnp.zeros((Q // devices, local_pairs), jnp.float32)

    def absorb(carry, piece):
        return (two_sum(carry, (piece, zeros)), None)

    summed, unused = lax.scan(absorb, (zeros, zeros), pieces)
    finished = (summed[0] + summed[1]) / total_blocks
    return lax.all_gather(finished, "tm", axis=0, tiled=True)


def solution(mesh):
    return jax.shard_map(
        shards,
        mesh=mesh,
        in_specs=(P(None, "tm"), P(("tm", "pair")), P(None, "pair")),
        out_specs=P(None, "pair"),
        check_vma=False,
    )
```

profile of v0, /device:TPU:0, one launch (start us, length us, event | category | flops | bytes accessed | tf_op | source)
XLA Modules:
  0.0 122.8 jit_solution(18230231065780740906)
XLA Ops:
  0.0 0.7 slice.73
  0.7 1.3 %collective-permute-start = (f32[2,256]{1,0:T(2,128)S(1)}, f32[2,256]{1,0:T(2,128)S(1)}, u32[]{:S(2)}, u32[]{:S(2)}) collective-permute-start(f32[2,256]{1,0:T(2,128)S(1)} %slice.73), channel_id=1, source_target_pairs={{4,0},{8,4},{12,8},{16,12},{20,16},{24,20},{28,24},{5,1},{9,5},{13... | collective-permute-start | bytes 6152 | tf_op jit(solution)/shard_map/ppermute | solution.py:16
  2.0 0.9 constant_dynamic-update-slice_fusion.1
  2.9 0.6 multiply_reduce_fusion
  3.9 1.2 %dynamic-slice = u32[1]{0:T(128)} dynamic-slice(u32[32]{0:T(128)} %constant.151, u32[]{:T(128)S(6)} %add.127), dynamic_slice_sizes={1} | dynamic-slice | bytes 12
  5.7 0.9 dynamic-update-slice
  6.5 6.4 %all-reduce.6 = s32[256]{0:T(256)S(1)} all-reduce(s32[256]{0:T(256)S(1)} %dynamic-update-slice), channel_id=1, replica_groups=mesh['tm'=8,'pair'=4] {'pair'}, use_global_device_ids=true, to_apply=%add.6 | all-reduce | flops 256 | bytes 2048
  13.7 1.1 fusion.35
  14.9 1.1 reshape.222
  16.0 0.3 fusion.46
  16.3 0.2 reshape.223
  16.5 0.2 reshape.224
  16.8 0.2 reshape.225
  17.0 0.2 reshape.226
  17.2 0.3 concatenate.90
  17.5 0.3 slice.100
  17.9 0.3 slice.101
  18.3 0.3 slice.102
  18.7 0.3 slice.103
  19.1 0.3 slice.104
  19.5 0.3 slice.105
  20.0 1.1 fusion.10
  21.1 1.3 %multiply_add_fusion.1 = (f32[256,256]{1,0:T(8,128)S(1)}, f32[256,256]{1,0:T(8,128)S(1)}) fusion(f32[256,512]{1,0:T(8,128)S(1)} %fusion.10, s32[256]{0:T(256)S(1)} %and_select_fusion), kind=kLoop, calls=%fused_computation.59 | loop fusion | flops 1310720 | bytes 1049600 | tf_op jit(solution)/shard_map/add | solution.py:78
  22.4 0.2 copy.10
  22.6 43.8 %while.23 = (s32[]{:T(128)}, f32[4,512,64]{2,1,0:T(8,128)}, s32[4,2,512]{2,1,0:T(2,128)}, f32[512,256]{1,0:T(8,128)S(1)}, f32[128,128]{1,0:T(8,128)S(1)}, /*index=5*/s32[]{:T(128)}, s32[]{:T(128)}, s32[]{}) while((s32[]{:T(128)}, f32[4,512,64]{2,1,0:T(8,128)}, s32[4,2,512]{2,1,0:T(2,128)}, f32[512,256]{1,0:T(8,128)S(1)}, ...), condition=%wide.region_3.4_spmd, body=%wide.region_1.3_spmd.sunk | while | flops 404751360 | bytes 17699432 | solution.py:126
  22.6 0.8 constant_dynamic-slice_fusion.3
  23.5 6.6 %gather_fusion = f32[2048,256]{1,0:T(8,128)S(1)} fusion(f32[512,256]{1,0:T(8,128)S(1)} %get-tuple-element.220, s32[2048]{0:T(1024)S(1)} %broadcast_clamp_fusion.2), kind=kCustom, calls=%fused_computation.clone.1 | custom fusion | bytes 4202496 | tf_op jit(solution)/shard_map/while/body/eval_jaxpr/jit(_take)/gather | solution.py:106
  30.1 0.3 broadcast_select_fusion.2
  30.8 0.3 copy.17
  31.2 0.2 copy.18
  31.4 0.3 copy.19
  31.7 1.1 fusion.54
  32.8 0.8 fusion.55
  33.6 0.8 constant_dynamic-slice_fusion.3
  34.4 6.6 %gather_fusion = f32[2048,256]{1,0:T(8,128)S(1)} fusion(f32[512,256]{1,0:T(8,128)S(1)} %get-tuple-element.220, s32[2048]{0:T(1024)S(1)} %broadcast_clamp_fusion.2), kind=kCustom, calls=%fused_computation.clone.1 | custom fusion | bytes 4202496 | tf_op jit(solution)/shard_map/while/body/eval_jaxpr/jit(_take)/gather | solution.py:106
  41.1 0.3 broadcast_select_fusion.2
  41.8 0.3 copy.17
  42.1 0.2 copy.18
  42.3 0.3 copy.19
  42.7 1.0 fusion.54
  43.7 0.8 fusion.55
  44.6 0.8 constant_dynamic-slice_fusion.3
  45.4 6.6 %gather_fusion = f32[2048,256]{1,0:T(8,128)S(1)} fusion(f32[512,256]{1,0:T(8,128)S(1)} %get-tuple-element.220, s32[2048]{0:T(1024)S(1)} %broadcast_clamp_fusion.2), kind=kCustom, calls=%fused_computation.clone.1 | custom fusion | bytes 4202496 | tf_op jit(solution)/shard_map/while/body/eval_jaxpr/jit(_take)/gather | solution.py:106
  52.0 0.3 broadcast_select_fusion.2
  52.7 0.3 copy.17
  53.1 0.2 copy.18
  53.3 0.3 copy.19
  53.6 1.1 fusion.54
  54.7 0.8 fusion.55
  55.5 0.8 constant_dynamic-slice_fusion.3
  56.3 6.6 %gather_fusion = f32[2048,256]{1,0:T(8,128)S(1)} fusion(f32[512,256]{1,0:T(8,128)S(1)} %get-tuple-element.220, s32[2048]{0:T(1024)S(1)} %broadcast_clamp_fusion.2), kind=kCustom, calls=%fused_computation.clone.1 | custom fusion | bytes 4202496 | tf_op jit(solution)/shard_map/while/body/eval_jaxpr/jit(_take)/gather | solution.py:106
  63.0 0.3 broadcast_select_fusion.2
  63.7 0.3 copy.17
  64.0 0.2 copy.18
  64.2 0.3 copy.19
  64.6 1.1 fusion.54
  65.6 0.8 fusion.55
  66.5 1.6 %copy.11 = f32[64,4,512]{2,1,0:T(4,128)S(1)} copy(f32[64,4,512]{0,2,1:T(8,128)} %bitcast.17) | data formatting | bytes 1048576 | tf_op jit(solution)/shard_map/transpose | solution.py:127
  68.1 1.2 all_to_all.6
  69.2 7.0 %all-to-all-start = ((f32[8,8,2048]{2,1,0:T(8,128)}), f32[8,8,2048]{2,1,0:T(8,128)S(1)}, u32[]{:S(2)}, u32[]{:S(2)}) async-start(f32[8,8,2048]{2,1,0:T(8,128)} %all_to_all.6), calls=%async_computation | async-start | bytes 1048576 | tf_op jit(solution)/shard_map/all_to_all | solution.py:130
  76.2 13.8 %all-to-all-done = f32[8,8,2048]{2,1,0:T(8,128)S(1)} async-done(((f32[8,8,2048]{2,1,0:T(8,128)}), f32[8,8,2048]{2,1,0:T(8,128)S(1)}, u32[]{:S(2)}, u32[]{:S(2)}) %all-to-all-start) | async-done | bytes 524320 | tf_op jit(solution)/shard_map/all_to_all | solution.py:130
  90.0 0.5 while.24
  90.5 31.6 %all_gather.7 = f32[64,2048]{1,0:T(8,128)S(1)} all-gather(f32[8,2048]{1,0:T(8,128)S(1)} %add_multiply_fusion), channel_id=1, replica_groups=mesh['tm'=8,'pair'=4] {'tm'}, dimensions={0}, use_global_device_ids=true | all-gather | bytes 589824 | tf_op jit(solution)/shard_map/all_gather | solution.py:139
  122.0 0.8 copy.39
  (54 shorter events, 3.2 us)
Async XLA Ops:
  0.7 15.3 %collective-permute-start = (f32[2,256]{1,0:T(2,128)S(1)}, f32[2,256]{1,0:T(2,128)S(1)}, u32[]{:S(2)}, u32[]{:S(2)}) collective-permute-start(f32[2,256]{1,0:T(2,128)S(1)} %slice.73), channel_id=1, source_target_pairs={{4,0},{8,4},{12,8},{16,12},{20,16},{24,20},{28,24},{5,1},{9,5},{13... | collective-permute-start | bytes 6152 | tf_op jit(solution)/shard_map/ppermute | solution.py:16
  69.2 20.8 %all-to-all-start = ((f32[8,8,2048]{2,1,0:T(8,128)}), f32[8,8,2048]{2,1,0:T(8,128)S(1)}, u32[]{:S(2)}, u32[]{:S(2)}) async-start(f32[8,8,2048]{2,1,0:T(8,128)} %all_to_all.6), calls=%async_computation | async-start | bytes 1048576 | tf_op jit(solution)/shard_map/all_to_all | solution.py:130
where the time goes:
time: 123 us
  local copies, waits for them, and re-layouts  45.5 us (37%)
  blocking collectives  38 us (31%)
  waiting for transfers between devices  13.8 us (11%)
  other arithmetic  10.1 us (8%)
  starting transfers between devices  8.23 us (7%)
  matrix products  5.25 us (4%)
  between operations  1.45 us (1%)
    all_gather x1, blocking collectives, shards(): return lax.all_gather(finished, 'tm', axis=0, tiled=True)  31.6 us
    gather x4, local copies, waits for them, and re-layouts, block_power(): picked = jnp.take(channel_major, columns, axis=0)  26.6 us
    all_to_all x1, waiting for transfers between devices, shards(): lax.all_to_all(partial_power, 'tm', split_axis=0, concat_axis=0, tiled=True)  13.8 us
    all_to_all x1, starting transfers between devices, shards(): lax.all_to_all(partial_power, 'tm', split_axis=0, concat_axis=0, tiled=True)  6.95 us
    unnamed x1, blocking collectives  6.41 us
    dot_general x4, matrix products, block_power(): jnp.einsum('qh,pbh->pbq', table, stacked, precision=lax.Precision.HIGHEST...  4.2 us
    unnamed x5, local copies, waits for them, and re-layouts  3.81 us
    dynamic_update_slice x4, other arithmetic, shards(): powers = lax.map(block_power, grouped)  3.36 us
  transfers between devices with their start and end apart: 2, of which 1 were waited for; matrix products, arithmetic and copies ran while one was open for 5% of the time, Pallas kernels for 0%

commit v1 on v0

v1 whole, which is shorter than its diff:
```python
import functools
import math

import jax
import jax.numpy as jnp
import numpy as np
from jax import lax
from jax.experimental import pallas as pl
from jax.experimental.pallas import tpu as pltpu
from jax.sharding import PartitionSpec as P

NP = 256
Q = 64
STRIDE = 64
SLOTS = NP // STRIDE
GROUP = Q // SLOTS
MESH = pl.DeviceIdType.MESH


def split_table(table):
    high = table.astype(jnp.bfloat16)
    low = (table - high.astype(np.float64)).astype(jnp.bfloat16)
    return high, low


def first_table():
    sample = np.arange(NP)
    angle = 2.0 * np.pi * (sample[:, None] * sample[None, :] % NP) / NP
    window = 0.54 - 0.46 * np.cos(2.0 * np.pi * sample / NP)
    gainval = 1.0 / np.sqrt(np.sum(window * window))
    return np.concatenate([np.cos(angle), np.sin(angle)], axis=0) * gainval


def hop_order():
    place = np.arange(Q)
    return place % GROUP * SLOTS + place // GROUP


def second_table():
    angle = 2.0 * np.pi * (np.arange(Q)[:, None] * hop_order()[None, :] % Q) / Q
    cosine = np.cos(angle) / math.sqrt(Q)
    sine = np.sin(angle) / math.sqrt(Q)
    upper = np.concatenate([cosine, sine], axis=1)
    lower = np.concatenate([-sine, cosine], axis=1)
    return np.concatenate([upper, lower], axis=0)


def parts_of(value):
    high = value.astype(jnp.bfloat16)
    return high, (value - high.astype(jnp.float32)).astype(jnp.bfloat16)


def dot(left, right):
    return jnp.dot(left, right, preferred_element_type=jnp.float32)


def kernel(
    devices, groups, chunks, width, total_blocks,
    signal, offsets, index, first_high, first_low, second_both, second_low,
    out,
    all_offsets, halo, spectra, partial, received, finished,
    offset_send, offset_recv, halo_send, halo_recv, part_send, part_recv, done_send, done_recv,
):
    me = lax.axis_index("tm")
    mine = lax.axis_index("pair")
    rows = signal.shape[1]
    blocks = rows // GROUP

    barrier = pltpu.get_barrier_semaphore()
    for step in range(1, devices):
        pl.semaphore_signal(barrier, inc=1, device_id={"tm": lax.rem(me + step, devices)}, device_id_type=MESH)
    for step in range(1, groups):
        pl.semaphore_signal(barrier, inc=1, device_id={"pair": lax.rem(mine + step, groups)}, device_id_type=MESH)
    pl.semaphore_wait(barrier, devices + groups - 2)

    edge = pltpu.make_async_remote_copy(
        src_ref=signal.at[:, 0:8, :], dst_ref=halo, send_sem=halo_send, recv_sem=halo_recv,
        device_id={"tm": lax.rem(me + devices - 1, devices)}, device_id_type=MESH,
    )
    edge.start()
    moves = []
    for step in range(1, groups):
        move = pltpu.make_async_remote_copy(
            src_ref=offsets, dst_ref=all_offsets.at[mine],
            send_sem=offset_send.at[step], recv_sem=offset_recv.at[step],
            device_id={"pair": lax.rem(mine + step, groups)}, device_id_type=MESH,
        )
        move.start()
        moves.append(move)
    all_offsets[mine] = offsets[...]
    for move in moves:
        move.wait()
    edge.wait()

    place = jnp.bitwise_and(all_offsets[...].reshape(rows, SLOTS), NP - 1)
    turn = place.astype(jnp.float32) * (2.0 * math.pi / NP)
    cosines = jnp.cos(turn) * 0.46
    sines = jnp.sin(turn) * 0.46
    sample = lax.broadcasted_iota(jnp.int32, (rows, NP), 1)
    around = lax.broadcasted_iota(jnp.int32, (1, NP), 1).astype(jnp.float32) * (2.0 * math.pi / NP)
    cosine_row = jnp.cos(around)
    sine_row = jnp.sin(around)
    keep = jnp.where(me == devices - 1, 0.0, 1.0)
    real = signal[0]
    imag = signal[1]
    real_next = jnp.concatenate([real[1:], halo[0, 0:1] * keep], axis=0)
    imag_next = jnp.concatenate([imag[1:], halo[1, 0:1] * keep], axis=0)
    for slot in range(SLOTS):
        where = place[:, slot : slot + 1]
        weight = 0.54 - (cosines[:, slot : slot + 1] * cosine_row + sines[:, slot : slot + 1] * sine_row)
        later = sample < where
        frame_re = jnp.where(later, real_next, real) * weight
        frame_im = jnp.where(later, imag_next, imag) * weight
        upper = jnp.concatenate([frame_re, frame_im], axis=1)
        lower = jnp.concatenate([frame_im, -frame_re], axis=1)
        high, low = parts_of(jnp.concatenate([upper, lower], axis=0))
        result = dot(high, first_high[...]) + dot(low, first_high[...]) + dot(high, first_low[...])
        high, low = parts_of(result)
        both = jnp.concatenate([high, low], axis=1)
        for block in range(blocks):
            at = block * Q + slot * GROUP
            for half in range(2):
                spectra[half * blocks * Q + at : half * blocks * Q + at + GROUP, :] = both[
                    half * rows + block * GROUP : half * rows + (block + 1) * GROUP
                ]

    channel = jnp.bitwise_and(lax.broadcasted_iota(jnp.int32, (2 * NP, width), 0), NP - 1)
    half_rows = blocks * Q
    part_moves = []
    done_moves = []

    def compute(chunk):
        columns = slice(chunk * width, (chunk + 1) * width)
        pick_first = jnp.where(channel == index[0:1, columns], 1.0, 0.0).astype(jnp.bfloat16)
        pick_second = jnp.where(channel == index[1:2, columns], 1.0, 0.0).astype(jnp.bfloat16)
        power = jnp.zeros((Q, width), jnp.float32)
        for block in range(blocks):
            re_rows = slice(block * Q, (block + 1) * Q)
            im_rows = slice(half_rows + block * Q, half_rows + (block + 1) * Q)
            wave = jnp.concatenate([spectra[re_rows, :], spectra[im_rows, :]], axis=0)
            first = dot(wave, pick_first)
            second = dot(wave, pick_second)
            product_re = first[:Q] * second[:Q] + first[Q:] * second[Q:]
            product_im = first[Q:] * second[:Q] - first[:Q] * second[Q:]
            high, low = parts_of(jnp.concatenate([product_re, product_im], axis=0))
            cyclic = dot(second_both[...], jnp.concatenate([high, low], axis=0)) + dot(second_low[...], high)
            squared = cyclic * cyclic
            power = power + (squared[:Q] + squared[Q:])
        share = Q // devices
        for device in range(devices):
            partial[chunk, device] = power[device * share : (device + 1) * share]
        for step in range(1, devices):
            to = lax.rem(me + step, devices)
            move = pltpu.make_async_remote_copy(
                src_ref=partial.at[chunk, to], dst_ref=received.at[chunk, step],
                send_sem=part_send.at[chunk, step], recv_sem=part_recv.at[chunk, step],
                device_id={"tm": to}, device_id_type=MESH,
            )
            move.start()
            part_moves.append((chunk, move))

    def reduce(chunk):
        columns = slice(chunk * width, (chunk + 1) * width)
        total = partial[chunk, me]
        for which, move in part_moves:
            if which == chunk:
                move.wait_recv()
        for step in range(1, devices):
            total = total + received[chunk, step]
        total = total * (1.0 / total_blocks)
        finished[chunk] = total
        out[me, :, columns] = total
        for step in range(1, devices):
            move = pltpu.make_async_remote_copy(
                src_ref=finished.at[chunk], dst_ref=out.at[me, :, columns],
                send_sem=done_send.at[chunk, step], recv_sem=done_recv.at[chunk, step],
                device_id={"tm": lax.rem(me + step, devices)}, device_id_type=MESH,
            )
            move.start()
            done_moves.append(move)

    for chunk in range(chunks):
        compute(chunk)
        if chunk >= 2:
            reduce(chunk - 2)
    for chunk in range(max(chunks - 2, 0), chunks):
        reduce(chunk)
    for which, move in part_moves:
        move.wait_send()
    for move in done_moves:
        move.wait()


def shards(devices, groups, signal, hop_offsets, pair_channels):
    span = signal.shape[1]
    rows = span // NP
    local_pairs = pair_channels.shape[1]
    width = math.gcd(local_pairs, 512)
    chunks = local_pairs // width
    share = Q // devices
    own_rows = hop_offsets.shape[0] // SLOTS
    blocks = rows // GROUP
    first_high, first_low = split_table(first_table())
    second_high, second_low = split_table(second_table())
    second_both = np.concatenate([second_high, second_high], axis=1)
    vmem = pl.BlockSpec(memory_space=pltpu.VMEM)
    dma = pltpu.SemaphoreType.DMA
    surface = pl.pallas_call(
        functools.partial(kernel, devices, groups, chunks, width, blocks * devices),
        out_shape=jax.ShapeDtypeStruct((devices, share, local_pairs), jnp.float32),
        in_specs=[vmem] * 7,
        out_specs=vmem,
        scratch_shapes=[
            pltpu.VMEM((groups, own_rows, SLOTS), jnp.int32),
            pltpu.VMEM((2, 8, NP), jnp.float32),
            pltpu.VMEM((2 * blocks * Q, 2 * NP), jnp.bfloat16),
            pltpu.VMEM((chunks, devices, share, width), jnp.float32),
            pltpu.VMEM((chunks, devices, share, width), jnp.float32),
            pltpu.VMEM((chunks, share, width), jnp.float32),
            dma((groups,)), dma((groups,)), dma, dma,
            dma((chunks, devices)), dma((chunks, devices)), dma((chunks, devices)), dma((chunks, devices)),
        ],
        compiler_params=pltpu.CompilerParams(collective_id=0, has_side_effects=True),
    )(
        signal.reshape(2, rows, NP), hop_offsets.reshape(own_rows, SLOTS), pair_channels,
        first_high, first_low, second_both, second_low,
    )
    return surface.reshape(Q, local_pairs)


def solution(mesh):
    return jax.shard_map(
        functools.partial(shards, mesh.shape["tm"], mesh.shape["pair"]),
        mesh=mesh,
        in_specs=(P(None, "tm"), P(("tm", "pair")), P(None, "pair")),
        out_specs=P(None, "pair"),
        check_vma=False,
    )
```

time: 123 us -> 43.2 us (0.35)
  local copies, waits for them, and re-layouts: 45.5 us -> 4.78 us
  Pallas kernels: 0 us -> 38.2 us
  blocking collectives: 38 us -> 0 us
  waiting for transfers between devices: 13.8 us -> 0 us
  other arithmetic: 10.1 us -> 0 us
  starting transfers between devices: 8.23 us -> 0 us
  matrix products: 5.25 us -> 0 us
  between operations: 1.45 us -> 0.01 us
    pallas_call x0 -> x1, Pallas kernels: none -> 38.2 us  [shards(): pl.pallas_call(functools.partial(kernel, devices, groups, chunks, width,...]
    all_gather x1 -> x0, blocking collectives: 31.6 us -> none  [shards(): return lax.all_gather(finished, 'tm', axis=0, tiled=True)]
    gather x4 -> x0, local copies, waits for them, and re-layouts: 26.6 us -> none  [block_power(): picked = jnp.take(channel_major, columns, axis=0)]
    all_to_all x1 -> x0, waiting for transfers between devices: 13.8 us -> none  [shards(): lax.all_to_all(partial_power, 'tm', split_axis=0, concat_axis=0, tiled=True)]
    all_to_all x1 -> x0, starting transfers between devices: 6.95 us -> none  [shards(): lax.all_to_all(partial_power, 'tm', split_axis=0, concat_axis=0, tiled=True)]
    unnamed x1 -> x0, blocking collectives: 6.41 us -> none
    slice x12 -> x0, local copies, waits for them, and re-layouts: 5.71 us -> none  [the longest x4 3.08 us: block_power(): index[0]]
    dot_general x5 -> x0, matrix products: 5.25 us -> none  [the longest x4 4.2 us: block_power(): jnp.einsum('qh,pbh->pbq', table, stacked, precision=lax.Precision.HIGHEST...]
  transfers between devices with their start and end apart: 2 -> 0, of which waited for: 1 -> 0; matrix products, arithmetic and copies ran while one was open for 5% -> 0% of each run, Pallas kernels for 0% -> 0%
where the time goes in v1:
time: 43.2 us; the launch traced here: 43 us
  Pallas kernels  38.2 us (88%)
  local copies, waits for them, and re-layouts  4.78 us (11%)
    pallas_call x1, Pallas kernels, shards(): pl.pallas_call(functools.partial(kernel, devices, groups, chunks, width,...  38.2 us
    unnamed x4, local copies, waits for them, and re-layouts  4.09 us

profile of v1, /device:TPU:0, one launch (start us, length us, event | category | flops | bytes accessed | tf_op | source)
XLA Modules:
  0.0 43.0 jit_solution(679050577733886287)
XLA Ops:
  0.0 0.0 copy-start
  0.0 0.7 %copy-done = s32[64]{0:T(128)S(1)} copy-done((s32[64]{0:T(128)S(1)}, s32[64]{0:T(128)}, u32[]{:S(2)}) %copy-start) | copy-done | bytes 280
  0.7 0.7 %reshape.10.offsets = s32[16,4]{1,0:T(8,128)} reshape(s32[64]{0:T(128)S(1)} %copy-done) | data formatting | bytes 512 | tf_op jit(solution)/shard_map/reshape | solution.py:225
  1.3 1.6 %copy.10 = f32[1,2,64,256]{3,2,1,0:T(8,128)} copy(f32[1,2,64,256]{3,1,2,0:T(2,128)} %bitcast.7) | data formatting | bytes 262144
  2.9 38.2 %shard_map.73 = f32[8,8,2048]{2,1,0:T(8,128)} custom-call(f32[2,64,256]{2,1,0:T(8,128)} %bitcast.6, s32[16,4]{1,0:T(8,128)} %reshape.10.offsets, s32[2,2048]{1,0:T(2,128)} %index.1, bf16[512,256]{1,0:T(8,128)(2,1)} %constant.8.clone.first_high, bf16[512,256]{1,0:T(8,128)(2,1)} %constant.9.clone.first_low, bf16[128,256]{1,0:T(8,128)(2,1)} %constant.10.clone.second_both, ...), custom_call_target="tpu_custom_call" | custom-call | tf_op jit(solution)/shard_map/pallas_call | solution.py:208
  41.1 1.9 %copy.12 = f32[64,2048]{1,0:T(8,128)} copy(f32[64,2048]{1,0:T(8,128)} %bitcast.5) | data formatting | bytes 1048576
Async XLA Ops:
  0.0 0.7 %copy-start = (s32[64]{0:T(128)S(1)}, s32[64]{0:T(128)}, u32[]{:S(2)}) copy-start(s32[64]{0:T(128)} %param.8) | copy-start | bytes 772

commit v2 on v1

--- a/solution.py
+++ b/solution.py
@@ -55,30 +55,66 @@
 
 
 def kernel(
-    devices, groups, chunks, width, total_blocks,
+    inner, outer, groups, chunks, width, total_blocks,
     signal, offsets, index, first_high, first_low, second_both, second_low,
     out,
-    all_offsets, halo, spectra, partial, received, finished,
-    offset_send, offset_recv, halo_send, halo_recv, part_send, part_recv, done_send, done_recv,
+    all_offsets, halo, spectra, partial, near, joined, far, finished,
+    offset_send, offset_recv, halo_send, halo_recv,
+    near_send, near_recv, far_send, far_recv, back_send, back_recv, done_send, done_recv,
 ):
     me = lax.axis_index("tm")
     mine = lax.axis_index("pair")
+    devices = inner * outer
+    across = lax.rem(me, inner)
+    along = me // inner
     rows = signal.shape[1]
     blocks = rows // GROUP
 
+    def near_peer(step):
+        place = lax.rem(across + step, inner)
+        return place, {"tm": along * inner + place}
+
+    def far_peer(step):
+        place = lax.rem(along + step, outer)
+        return place, {"tm": place * inner + across}
+
     barrier = pltpu.get_barrier_semaphore()
-    for step in range(1, devices):
-        pl.semaphore_signal(barrier, inc=1, device_id={"tm": lax.rem(me + step, devices)}, device_id_type=MESH)
+
+    def greet(device):
+        pl.semaphore_signal(barrier, inc=1, device_id=device, device_id_type=MESH)
+
+    for step in range(1, inner):
+        greet(near_peer(step)[1])
+    for step in range(1, outer):
+        greet(far_peer(step)[1])
     for step in range(1, groups):
-        pl.semaphore_signal(barrier, inc=1, device_id={"pair": lax.rem(mine + step, groups)}, device_id_type=MESH)
-    pl.semaphore_wait(barrier, devices + groups - 2)
+        greet({"pair": lax.rem(mine + step, groups)})
+
+    @pl.when(me > 0)
+    def _():
+        greet({"tm": me - 1})
+
+    @pl.when(me < devices - 1)
+    def _():
+        greet({"tm": me + 1})
+
+    ends = jnp.where(me > 0, 1, 0) + jnp.where(me < devices - 1, 1, 0)
+    pl.semaphore_wait(barrier, inner + outer + groups - 3 + ends)
 
     edge = pltpu.make_async_remote_copy(
         src_ref=signal.at[:, 0:8, :], dst_ref=halo, send_sem=halo_send, recv_sem=halo_recv,
         device_id={"tm": lax.rem(me + devices - 1, devices)}, device_id_type=MESH,
     )
-    edge.start()
-    moves = []
+
+    @pl.when(me > 0)
+    def _():
+        edge.start()
+
+    @pl.when(me == devices - 1)
+    def _():
+        halo[...] = jnp.zeros_like(halo)
+
+    hellos = []
     for step in range(1, groups):
         move = pltpu.make_async_remote_copy(
             src_ref=offsets, dst_ref=all_offsets.at[mine],
@@ -86,11 +122,18 @@
             device_id={"pair": lax.rem(mine + step, groups)}, device_id_type=MESH,
         )
         move.start()
-        moves.append(move)
+        hellos.append(move)
     all_offsets[mine] = offsets[...]
-    for move in moves:
+    for move in hellos:
         move.wait()
-    edge.wait()
+
+    @pl.when(me > 0)
+    def _():
+        edge.wait_send()
+
+    @pl.when(me < devices - 1)
+    def _():
+        edge.wait_recv()
 
     place = jnp.bitwise_and(all_offsets[...].reshape(rows, SLOTS), NP - 1)
     turn = place.astype(jnp.float32) * (2.0 * math.pi / NP)
@@ -100,11 +143,10 @@
     around = lax.broadcasted_iota(jnp.int32, (1, NP), 1).astype(jnp.float32) * (2.0 * math.pi / NP)
     cosine_row = jnp.cos(around)
     sine_row = jnp.sin(around)
-    keep = jnp.where(me == devices - 1, 0.0, 1.0)
     real = signal[0]
     imag = signal[1]
-    real_next = jnp.concatenate([real[1:], halo[0, 0:1] * keep], axis=0)
-    imag_next = jnp.concatenate([imag[1:], halo[1, 0:1] * keep], axis=0)
+    real_next = jnp.concatenate([real[1:], halo[0, 0:1]], axis=0)
+    imag_next = jnp.concatenate([imag[1:], halo[1, 0:1]], axis=0)
     for slot in range(SLOTS):
         where = place[:, slot : slot + 1]
         weight = 0.54 - (cosines[:, slot : slot + 1] * cosine_row + sines[:, slot : slot + 1] * sine_row)
@@ -126,8 +168,20 @@
 
     channel = jnp.bitwise_and(lax.broadcasted_iota(jnp.int32, (2 * NP, width), 0), NP - 1)
     half_rows = blocks * Q
-    part_moves = []
-    done_moves = []
+    share = Q // devices
+    moves = {}
+
+    def send(name, chunk, step, source, target, sems, device):
+        move = pltpu.make_async_remote_copy(
+            src_ref=source, dst_ref=target, send_sem=sems[0].at[chunk, step], recv_sem=sems[1].at[chunk, step],
+            device_id=device, device_id_type=MESH,
+        )
+        move.start()
+        moves.setdefault((name, chunk), []).append(move)
+
+    def arrive(name, chunk):
+        for move in moves.get((name, chunk), []):
+            move.wait_recv()
 
     def compute(chunk):
         columns = slice(chunk * width, (chunk + 1) * width)
@@ -146,57 +200,64 @@
             cyclic = dot(second_both[...], jnp.concatenate([high, low], axis=0)) + dot(second_low[...], high)
             squared = cyclic * cyclic
             power = power + (squared[:Q] + squared[Q:])
-        share = Q // devices
-        for device in range(devices):
-            partial[chunk, device] = power[device * share : (device + 1) * share]
-        for step in range(1, devices):
-            to = lax.rem(me + step, devices)
-            move = pltpu.make_async_remote_copy(
-                src_ref=partial.at[chunk, to], dst_ref=received.at[chunk, step],
-                send_sem=part_send.at[chunk, step], recv_sem=part_recv.at[chunk, step],
-                device_id={"tm": to}, device_id_type=MESH,
-            )
-            move.start()
-            part_moves.append((chunk, move))
-
-    def reduce(chunk):
+        for place in range(inner):
+            for other in range(outer):
+                at = (place * outer + other) * share
+                partial[chunk, place, other] = power[at : at + share]
+        for step in range(1, inner):
+            place, device = near_peer(step)
+            send("near", chunk, step, partial.at[chunk, place], near.at[chunk, step], (near_send, near_recv), device)
+
+    def join(chunk):
+        total = partial[chunk, across]
+        arrive("near", chunk)
+        for step in range(1, inner):
+            total = total + near[chunk, step]
+        joined[chunk] = total
+        for step in range(1, outer):
+            place, device = far_peer(step)
+            send("far", chunk, step, joined.at[chunk, place], far.at[chunk, step], (far_send, far_recv), device)
+
+    def finish(chunk):
         columns = slice(chunk * width, (chunk + 1) * width)
-        total = partial[chunk, me]
-        for which, move in part_moves:
-            if which == chunk:
-                move.wait_recv()
-        for step in range(1, devices):
-            total = total + received[chunk, step]
+        total = joined[chunk, along]
+        arrive("far", chunk)
+        for step in range(1, outer):
+            total = total + far[chunk, step]
         total = total * (1.0 / total_blocks)
         finished[chunk] = total
-        out[me, :, columns] = total
-        for step in range(1, devices):
-            move = pltpu.make_async_remote_copy(
-                src_ref=finished.at[chunk], dst_ref=out.at[me, :, columns],
-                send_sem=done_send.at[chunk, step], recv_sem=done_recv.at[chunk, step],
-                device_id={"tm": lax.rem(me + step, devices)}, device_id_type=MESH,
-            )
-            move.start()
-            done_moves.append(move)
-
+        out[across, along, :, columns] = total
+        for step in range(1, outer):
+            target = out.at[across, along, :, columns]
+            send("back", chunk, step, finished.at[chunk], target, (back_send, back_recv), far_peer(step)[1])
+
+    def spread(chunk):
+        columns = slice(chunk * width, (chunk + 1) * width)
+        arrive("back", chunk)
+        for step in range(1, inner):
+            line = out.at[across, :, :, columns]
+            send("done", chunk, step, line, line, (done_send, done_recv), near_peer(step)[1])
+
+    stages = ((compute, 0), (join, 3), (finish, 6), (spread, 9))
+    for tick in range(chunks + stages[-1][1]):
+        for stage, lag in stages:
+            if 0 <= tick - lag < chunks:
+                stage(tick - lag)
     for chunk in range(chunks):
-        compute(chunk)
-        if chunk >= 2:
-            reduce(chunk - 2)
-    for chunk in range(max(chunks - 2, 0), chunks):
-        reduce(chunk)
-    for which, move in part_moves:
-        move.wait_send()
-    for move in done_moves:
-        move.wait()
+        arrive("done", chunk)
+    for group in moves.values():
+        for move in group:
+            move.wait_send()
 
 
 def shards(devices, groups, signal, hop_offsets, pair_channels):
     span = signal.shape[1]
     rows = span // NP
     local_pairs = pair_channels.shape[1]
-    width = math.gcd(local_pairs, 512)
+    width = math.gcd(local_pairs, 256)
     chunks = local_pairs // width
+    inner = 1 << (devices.bit_length() - 1) // 2
+    outer = devices // inner
     share = Q // devices
     own_rows = hop_offsets.shape[0] // SLOTS
     blocks = rows // GROUP
@@ -206,19 +267,22 @@
     vmem = pl.BlockSpec(memory_space=pltpu.VMEM)
     dma = pltpu.SemaphoreType.DMA
     surface = pl.pallas_call(
-        functools.partial(kernel, devices, groups, chunks, width, blocks * devices),
-        out_shape=jax.ShapeDtypeStruct((devices, share, local_pairs), jnp.float32),
+        functools.partial(kernel, inner, outer, groups, chunks, width, blocks * devices),
+        out_shape=jax.ShapeDtypeStruct((inner, outer, share, local_pairs), jnp.float32),
         in_specs=[vmem] * 7,
         out_specs=vmem,
         scratch_shapes=[
             pltpu.VMEM((groups, own_rows, SLOTS), jnp.int32),
             pltpu.VMEM((2, 8, NP), jnp.float32),
             pltpu.VMEM((2 * blocks * Q, 2 * NP), jnp.bfloat16),
-            pltpu.VMEM((chunks, devices, share, width), jnp.float32),
-            pltpu.VMEM((chunks, devices, share, width), jnp.float32),
+            pltpu.VMEM((chunks, inner, outer, share, width), jnp.float32),
+            pltpu.VMEM((chunks, inner, outer, share, width), jnp.float32),
+            pltpu.VMEM((chunks, outer, share, width), jnp.float32),
+            pltpu.VMEM((chunks, outer, share, width), jnp.float32),
             pltpu.VMEM((chunks, share, width), jnp.float32),
             dma((groups,)), dma((groups,)), dma, dma,
-            dma((chunks, devices)), dma((chunks, devices)), dma((chunks, devices)), dma((chunks, devices)),
+            dma((chunks, inner)), dma((chunks, inner)), dma((chunks, outer)), dma((chunks, outer)),
+            dma((chunks, outer)), dma((chunks, outer)), dma((chunks, inner)), dma((chunks, inner)),
         ],
         compiler_params=pltpu.CompilerParams(collective_id=0, has_side_effects=True),
     )(

time: 43.2 us -> 43.2 us (level)
  no operation moved by 1% of the time
where the time goes in v2:
time: 43.2 us; the launch traced here: 43 us
  Pallas kernels  38.2 us (88%)
  local copies, waits for them, and re-layouts  4.78 us (11%)
    pallas_call x1, Pallas kernels, shards(): pl.pallas_call(functools.partial(kernel, inner, outer, groups, chunks, wi...  38.2 us
    unnamed x4, local copies, waits for them, and re-layouts  4.09 us

profile of v2, /device:TPU:0, one launch (start us, length us, event | category | flops | bytes accessed | tf_op | source)
XLA Modules:
  0.0 43.0 jit_solution(4965512942515551393)
XLA Ops:
  0.0 0.0 copy-start
  0.0 0.7 %copy-done = s32[64]{0:T(128)S(1)} copy-done((s32[64]{0:T(128)S(1)}, s32[64]{0:T(128)}, u32[]{:S(2)}) %copy-start) | copy-done | bytes 280
  0.7 0.7 %reshape.10.offsets = s32[16,4]{1,0:T(8,128)} reshape(s32[64]{0:T(128)S(1)} %copy-done) | data formatting | bytes 512 | tf_op jit(solution)/shard_map/reshape | solution.py:289
  1.3 1.6 %copy.10 = f32[1,2,64,256]{3,2,1,0:T(8,128)} copy(f32[1,2,64,256]{3,1,2,0:T(2,128)} %bitcast.7) | data formatting | bytes 262144
  2.9 38.2 %shard_map.73 = f32[2,4,8,2048]{3,2,1,0:T(8,128)} custom-call(f32[2,64,256]{2,1,0:T(8,128)} %bitcast.6, s32[16,4]{1,0:T(8,128)} %reshape.10.offsets, s32[2,2048]{1,0:T(2,128)} %index.1, bf16[512,256]{1,0:T(8,128)(2,1)} %constant.8.clone.first_high, bf16[512,256]{1,0:T(8,128)(2,1)} %constant.9.clone.first_low, bf16[128,256]{1,0:T(8,128)(2,1)} %constant.10.clone.second_both, ...), custom_call_target="tpu_custom_call" | custom-call | tf_op jit(solution)/shard_map/pallas_call | solution.py:269
  41.1 1.9 %copy.12 = f32[64,2048]{1,0:T(8,128)} copy(f32[64,2048]{1,0:T(8,128)} %bitcast.5) | data formatting | bytes 1048576
Async XLA Ops:
  0.0 0.7 %copy-start = (s32[64]{0:T(128)S(1)}, s32[64]{0:T(128)}, u32[]{:S(2)}) copy-start(s32[64]{0:T(128)} %param.8) | copy-start | bytes 772

commit v3 on v2

--- a/solution.py
+++ b/solution.py
@@ -58,7 +58,7 @@
     inner, outer, groups, chunks, width, total_blocks,
     signal, offsets, index, first_high, first_low, second_both, second_low,
     out,
-    all_offsets, halo, spectra, partial, near, joined, far, finished,
+    samples, all_offsets, halo, spectra, partial, near, joined, far, finished,
     offset_send, offset_recv, halo_send, halo_recv,
     near_send, near_recv, far_send, far_recv, back_send, back_recv, done_send, done_recv,
 ):
@@ -67,7 +67,7 @@
     devices = inner * outer
     across = lax.rem(me, inner)
     along = me // inner
-    rows = signal.shape[1]
+    rows = samples.shape[1]
     blocks = rows // GROUP
 
     def near_peer(step):
@@ -98,11 +98,14 @@
     def _():
         greet({"tm": me + 1})
 
+    for row in range(rows):
+        samples[:, row, :] = signal[:, row * NP : (row + 1) * NP]
+
     ends = jnp.where(me > 0, 1, 0) + jnp.where(me < devices - 1, 1, 0)
     pl.semaphore_wait(barrier, inner + outer + groups - 3 + ends)
 
     edge = pltpu.make_async_remote_copy(
-        src_ref=signal.at[:, 0:8, :], dst_ref=halo, send_sem=halo_send, recv_sem=halo_recv,
+        src_ref=signal.at[:, 0:NP], dst_ref=halo, send_sem=halo_send, recv_sem=halo_recv,
         device_id={"tm": lax.rem(me + devices - 1, devices)}, device_id_type=MESH,
     )
 
@@ -135,18 +138,32 @@
     def _():
         edge.wait_recv()
 
-    place = jnp.bitwise_and(all_offsets[...].reshape(rows, SLOTS), NP - 1)
-    turn = place.astype(jnp.float32) * (2.0 * math.pi / NP)
+    own_hops = offsets.shape[1]
+    own_rows = own_hops // SLOTS
+    hop = lax.broadcasted_iota(jnp.int32, (own_rows, own_hops), 1)
+    first_hop = lax.broadcasted_iota(jnp.int32, (own_rows, own_hops), 0) * SLOTS
+    lane = lax.broadcasted_iota(jnp.int32, (own_rows, SLOTS), 1)
+    places = []
+    for group in range(groups):
+        line = jnp.bitwise_and(all_offsets[group], NP - 1).astype(jnp.float32)
+        place = jnp.zeros((own_rows, SLOTS), jnp.float32)
+        for slot in range(SLOTS):
+            chosen = jnp.where(hop == first_hop + slot, line, 0.0)
+            place = jnp.where(lane == slot, jnp.sum(chosen, axis=1, keepdims=True), place)
+        places.append(place)
+    place = jnp.concatenate(places, axis=0)
+    turn = place * (2.0 * math.pi / NP)
+    place = place.astype(jnp.int32)
     cosines = jnp.cos(turn) * 0.46
     sines = jnp.sin(turn) * 0.46
     sample = lax.broadcasted_iota(jnp.int32, (rows, NP), 1)
     around = lax.broadcasted_iota(jnp.int32, (1, NP), 1).astype(jnp.float32) * (2.0 * math.pi / NP)
     cosine_row = jnp.cos(around)
     sine_row = jnp.sin(around)
-    real = signal[0]
-    imag = signal[1]
-    real_next = jnp.concatenate([real[1:], halo[0, 0:1]], axis=0)
-    imag_next = jnp.concatenate([imag[1:], halo[1, 0:1]], axis=0)
+    real = samples[0]
+    imag = samples[1]
+    real_next = jnp.concatenate([real[1:], halo[0:1]], axis=0)
+    imag_next = jnp.concatenate([imag[1:], halo[1:2]], axis=0)
     for slot in range(SLOTS):
         where = place[:, slot : slot + 1]
         weight = 0.54 - (cosines[:, slot : slot + 1] * cosine_row + sines[:, slot : slot + 1] * sine_row)
@@ -238,7 +255,7 @@
             line = out.at[across, :, :, columns]
             send("done", chunk, step, line, line, (done_send, done_recv), near_peer(step)[1])
 
-    stages = ((compute, 0), (join, 3), (finish, 6), (spread, 9))
+    stages = ((compute, 0), (join, 1), (finish, 2), (spread, 3))
     for tick in range(chunks + stages[-1][1]):
         for stage, lag in stages:
             if 0 <= tick - lag < chunks:
@@ -254,7 +271,7 @@
     span = signal.shape[1]
     rows = span // NP
     local_pairs = pair_channels.shape[1]
-    width = math.gcd(local_pairs, 256)
+    width = math.gcd(local_pairs, 512)
     chunks = local_pairs // width
     inner = 1 << (devices.bit_length() - 1) // 2
     outer = devices // inner
@@ -272,8 +289,9 @@
         in_specs=[vmem] * 7,
         out_specs=vmem,
         scratch_shapes=[
-            pltpu.VMEM((groups, own_rows, SLOTS), jnp.int32),
-            pltpu.VMEM((2, 8, NP), jnp.float32),
+            pltpu.VMEM((2, rows, NP), jnp.float32),
+            pltpu.VMEM((groups, 1, own_rows * SLOTS), jnp.int32),
+            pltpu.VMEM((2, NP), jnp.float32),
             pltpu.VMEM((2 * blocks * Q, 2 * NP), jnp.bfloat16),
             pltpu.VMEM((chunks, inner, outer, share, width), jnp.float32),
             pltpu.VMEM((chunks, inner, outer, share, width), jnp.float32),
@@ -286,7 +304,7 @@
         ],
         compiler_params=pltpu.CompilerParams(collective_id=0, has_side_effects=True),
     )(
-        signal.reshape(2, rows, NP), hop_offsets.reshape(own_rows, SLOTS), pair_channels,
+        signal, hop_offsets.reshape(1, own_rows * SLOTS), pair_channels,
         first_high, first_low, second_both, second_low,
     )
     return surface.reshape(Q, local_pairs)

time: 43.2 us -> 38.6 us (0.89)
  local copies, waits for them, and re-layouts: 4.78 us -> 1.87 us
  Pallas kernels: 38.2 us -> 36.6 us
    unnamed x4 -> x1, local copies, waits for them, and re-layouts: 4.09 us -> 1.87 us
    pallas_call x1, Pallas kernels: 38.2 us -> 36.6 us  [shards(): pl.pallas_call(functools.partial(kernel, inner, outer, groups, chunks, wi...]
    reshape x1 -> x0, local copies, waits for them, and re-layouts: 0.68 us -> none  [shards(): hop_offsets.reshape(own_rows, SLOTS)]
where the time goes in v3:
time: 38.6 us; the launch traced here: 38.4 us
  Pallas kernels  36.6 us (95%)
  local copies, waits for them, and re-layouts  1.87 us (5%)
    pallas_call x1, Pallas kernels, shards(): pl.pallas_call(functools.partial(kernel, inner, outer, groups, chunks, wi...  36.6 us
    unnamed x1, local copies, waits for them, and re-layouts  1.87 us

profile of v3, /device:TPU:0, one launch (start us, length us, event | category | flops | bytes accessed | tf_op | source)
XLA Modules:
  0.0 38.4 jit_solution(3099485803900847782)
XLA Ops:
  0.0 36.6 %shard_map.73 = f32[2,4,8,2048]{3,2,1,0:T(8,128)} custom-call(f32[2,16384]{1,0:T(2,128)} %signal.1, s32[1,64]{1,0:T(1,128)} %bitcast.3, s32[2,2048]{1,0:T(2,128)} %index.1, bf16[512,256]{1,0:T(8,128)(2,1)} %constant.8.clone.first_high, bf16[512,256]{1,0:T(8,128)(2,1)} %constant.9.clone.first_low, bf16[128,256]{1,0:T(8,128)(2,1)} %constant.10.clone.second_both, ...), custom_call_target="tpu_custom_call" | custom-call | tf_op jit(solution)/shard_map/pallas_call | solution.py:286
  36.6 1.9 %copy.9 = f32[64,2048]{1,0:T(8,128)} copy(f32[64,2048]{1,0:T(8,128)} %bitcast.2) | data formatting | bytes 1048576
